TPU v7x, 32 devices: a whole 2x2x4 slice. The times are simulated.
32 devices in a mesh: grp: 4 (over y, core), dev: 8 (over z, x).
Axes of the slice: x: 2, y: 2, z: 4, core: 2. Of those that a mesh axis runs over, the one named last changes fastest.
Arguments:
- basis_values: bfloat16 [128, 256, 512], P(('grp', 'dev')), may hold values from -1 to 1
- stored_density_blocks: bfloat16 [64, 128, 128], P('dev'), may hold values from -0.5 to 0.5
- device_request: int32 [32, 8, 8], P(('grp', 'dev')), may hold values from -1 to 7, as said below
- batch_blocks: int32 [128, 16], P(('grp', 'dev')), may hold values from 0 to 63, as said below
- batch_atom: int32 [128], P(('grp', 'dev')), may hold values from 0 to 999
- point_offset: float32 [3, 128, 256], P(None, ('grp', 'dev')), may hold values from -8 to 8
- point_weight: float32 [128, 256], P(('grp', 'dev')), may hold values from 0.02 to 0.5
- exchange_kernel: float32 [128, 256], P(('grp', 'dev')), may hold values from -3 to -0.3
- atom_xyz: float32 [3, 1000], replicated, may hold values from -15 to 15
Outputs:
- response_hamiltonian: bfloat16 [64, 128, 128], P('dev')
- response_density: float32 [128, 256], P(('grp', 'dev'))
- multipoles: float32 [4, 1000], replicated
Inputs may be any that keep to these rules, and one draw needn't show every extreme that they name: `device_request`: row d belongs to device d of grp+dev in grp-major order. Each row has exactly 32 entries other than -1, distinct for one owner; in every group one owner is asked for 8 blocks by every device of the group. `batch_blocks`: every entry points to an entry of its device's request row that is not -1.
All inputs are finite; a program needn't handle non-finite values.
Results may differ from a plain program's by a relative error of at most 0.004.
Values may be sent and summed in bfloat16 or wider, within the bound.
A program may use at most 64 MiB of HBM per device.

v0:
```python
import jax
import jax.numpy as jnp
from jax import lax
from jax.sharding import PartitionSpec as P

HIGH = lax.Precision.HIGHEST


def far_field(multipoles, centre, offset, atom_xyz):
    gap = centre[:, None, None] + offset[:, :, None] - atom_xyz[:, None, :]
    inverse = lax.rsqrt(gap[0] * gap[0] + gap[1] * gap[1] + gap[2] * gap[2] + 1.0)
    cube = inverse * inverse * inverse
    dipole = multipoles[1] * gap[0] + multipoles[2] * gap[1] + multipoles[3] * gap[2]
    return jnp.sum(multipoles[0] * inverse + dipole * cube, axis=1)


def scaled_rows(values, factor):
    return (values.astype(jnp.float32) * factor[:, None]).astype(jnp.bfloat16)


def pair_terms(scaled, values, rel, tile):
    points = values.shape[0]
    return jnp.einsum(
        "rim,rjn->ijmn",
        scaled.reshape(-1, rel, tile),
        values.reshape(points, rel, tile),
        preferred_element_type=jnp.float32,
    )


def on_device(
    basis_values,
    stored_density_blocks,
    device_request,
    batch_blocks,
    batch_atom,
    point_offset,
    point_weight,
    exchange_kernel,
    atom_xyz,
):
    batches, points, width = basis_values.shape
    own, tile = (stored_density_blocks.shape[0], stored_density_blocks.shape[1])
    rel = width // tile
    wanted = device_request[0]
    owners, capacity = wanted.shape
    positions = owners * capacity
    atoms = atom_xyz.shape[1]
    picked = jnp.take(
        stored_density_blocks,
        jnp.clip(
            lax.all_to_all(wanted, "dev", split_axis=0, concat_axis=0, tiled=True), 0, own - 1
        ),
        axis=0,
    )
    fetched = lax.all_to_all(picked, "dev", split_axis=0, concat_axis=0, tiled=True)
    fetched = fetched.reshape(positions, tile, tile)

    def density_one(args):
        values, needed = args
        blocks = jnp.take(fetched, needed, axis=0).reshape(rel, rel, tile, tile)
        split = values.reshape(points, rel, tile)
        left = jnp.einsum("rim,ijmn->rijn", split, blocks, preferred_element_type=jnp.float32)
        return jnp.einsum("rijn,rjn->r", left, split.astype(jnp.float32))

    density_field = lax.map(density_one, (basis_values, batch_blocks))
    weighted = density_field * point_weight
    local_parts = jnp.stack(
        [
            jnp.sum(weighted, 1),
            jnp.sum(weighted * point_offset[0], 1),
            jnp.sum(weighted * point_offset[1], 1),
            jnp.sum(weighted * point_offset[2], 1),
        ]
    )
    onehot = (batch_atom[:, None] == jnp.arange(atoms, dtype=jnp.int32)[None, :]).astype(
        jnp.float32
    )
    local_moments = jnp.dot(local_parts, onehot, precision=HIGH)
    centres = jnp.dot(atom_xyz, onehot.T, precision=HIGH)
    xc_part = point_weight * exchange_kernel * density_field
    multipoles = lax.psum(local_moments, ("grp", "dev"))

    def potential_one(args):
        centre, offset = args
        return far_field(multipoles, centre, offset, atom_xyz)

    hartree_part = point_weight * lax.map(
        potential_one, (centres.T, jnp.moveaxis(point_offset, 1, 0))
    )

    def both_one(args):
        values, first, second = args
        stacked = jnp.concatenate([scaled_rows(values, first), scaled_rows(values, second)], axis=0)
        doubled = jnp.concatenate([values, values], axis=0)
        return pair_terms(stacked, doubled, rel, tile)

    terms = lax.map(both_one, (basis_values, xc_part, hartree_part))
    flat_terms = terms.reshape(batches * rel * rel, tile * tile)
    summed = jax.ops.segment_sum(flat_terms, batch_blocks.reshape(-1), num_segments=positions)
    outgoing = summed.astype(jnp.bfloat16).reshape(owners, capacity, tile, tile)
    received, received_ids = (
        lax.all_to_all(outgoing, "dev", split_axis=0, concat_axis=0, tiled=True),
        lax.all_to_all(wanted, "dev", split_axis=0, concat_axis=0, tiled=True),
    )
    owner_onehot = (
        jnp.arange(own, dtype=jnp.int32)[:, None] == received_ids.reshape(1, positions)
    ).astype(jnp.bfloat16)
    owned = jnp.dot(
        owner_onehot, received.reshape(positions, tile * tile), preferred_element_type=jnp.float32
    )
    total = lax.psum(owned, "grp")
    hamiltonian = total.astype(jnp.bfloat16).reshape(own, tile, tile)
    return (hamiltonian, density_field, multipoles)


def solution(mesh):
    return jax.shard_map(
        on_device,
        mesh=mesh,
        in_specs=(
            P(("grp", "dev"), None, None),
            P("dev", None, None),
            P(("grp", "dev"), None, None),
            P(("grp", "dev"), None),
            P(("grp", "dev")),
            P(None, ("grp", "dev"), None),
            P(("grp", "dev"), None),
            P(("grp", "dev"), None),
            P(),
        ),
        out_specs=(P("dev", None, None), P(("grp", "dev"), None), P()),
        check_vma=False,
    )
```

profile of v0, /device:TPU:0, one launch (start us, length us, event | category | flops | bytes accessed | tf_op | source)
XLA Modules:
  0.0 220.7 jit_solution(17259196471486747598)
XLA Ops:
  0.6 13.8 %all_to_all.20 = s32[8,1,8]{2,1,0:T(1,128)S(1)} all-to-all(s32[8,1,8]{2,1,0:T(1,128)} %bitcast.168), channel_id=1, replica_groups=mesh['grp'=4,'dev'=8] {'dev'}, dimensions={0} | all-to-all | bytes 512 | tf_op jit(solution)/shard_map/all_to_all | solution.py:104
  14.6 1.0 gather_fusion.1
  15.6 1.6 broadcast_select_fusion
  17.2 4.5 %all-to-all-start.1 = ((bf16[8,8,128,128]{3,2,1,0:T(8,128)(2,1)}), bf16[8,8,128,128]{3,2,1,0:T(8,128)(2,1)}, u32[]{:S(2)}, u32[]{:S(2)}) async-start(bf16[8,8,128,128]{3,2,1,0:T(8,128)(2,1)} %broadcast_select_fusion), calls=%async_computation.1 | async-start | bytes 4194304 | tf_op jit(solution)/shard_map/all_to_all | solution.py:56
  21.8 0.5 copy.53
  22.5 46.2 %all-to-all-done.1 = bf16[8,8,128,128]{3,2,1,0:T(8,128)(2,1)} async-done(((bf16[8,8,128,128]{3,2,1,0:T(8,128)(2,1)}), bf16[8,8,128,128]{3,2,1,0:T(8,128)(2,1)}, u32[]{:S(2)}, u32[]{:S(2)}) %all-to-all-start.1) | async-done | bytes 2097184 | tf_op jit(solution)/shard_map/all_to_all | solution.py:56
  68.8 12.6 %while.30 = (s32[]{:T(128)}, f32[4,256]{1,0:T(4,128)S(1)}, bf16[4,256,512]{1,2,0:T(8,128)(2,1)S(1)}, s32[4,16]{1,0:T(4,128)S(1)}, bf16[64,128,128]{2,1,0:T(8,128)(2,1)}, /*index=5*/s32[]{:T(128)}, s32[]{:T(128)}) while((s32[]{:T(128)}, f32[4,256]{1,0:T(4,128)S(1)}, bf16[4,256,512]{1,2,0:T(8,128)(2,1)S(1)}, s32[4,16]{1,0:T(4,128)S(1)}, ...), condition=%wide.region_1.2_spmd, body=%wide.region_0.1_spmd.sunk | while | flops 134874000 | bytes 2629349 | solution.py:66
  69.0 2.2 %gather_fusion = bf16[16,128,128]{2,1,0:T(8,128)(2,1)S(1)} fusion(bf16[64,128,128]{2,1,0:T(8,128)(2,1)} %get-tuple-element.346, s32[1024]{0:T(1024)S(1)} %pad_clamp_fusion.3), kind=kCustom, calls=%fused_computation.clone.1 | custom fusion | bytes 1048640 | tf_op jit(solution)/shard_map/while/body/eval_jaxpr/jit(_take)/gather | solution.py:61
  71.3 0.6 fusion.53
  72.2 2.2 %gather_fusion = bf16[16,128,128]{2,1,0:T(8,128)(2,1)S(1)} fusion(bf16[64,128,128]{2,1,0:T(8,128)(2,1)} %get-tuple-element.346, s32[1024]{0:T(1024)S(1)} %pad_clamp_fusion.3), kind=kCustom, calls=%fused_computation.clone.1 | custom fusion | bytes 1048640 | tf_op jit(solution)/shard_map/while/body/eval_jaxpr/jit(_take)/gather | solution.py:61
  74.4 0.6 fusion.53
  75.3 2.2 %gather_fusion = bf16[16,128,128]{2,1,0:T(8,128)(2,1)S(1)} fusion(bf16[64,128,128]{2,1,0:T(8,128)(2,1)} %get-tuple-element.346, s32[1024]{0:T(1024)S(1)} %pad_clamp_fusion.3), kind=kCustom, calls=%fused_computation.clone.1 | custom fusion | bytes 1048640 | tf_op jit(solution)/shard_map/while/body/eval_jaxpr/jit(_take)/gather | solution.py:61
  77.6 0.6 fusion.53
  78.5 2.2 %gather_fusion = bf16[16,128,128]{2,1,0:T(8,128)(2,1)S(1)} fusion(bf16[64,128,128]{2,1,0:T(8,128)(2,1)} %get-tuple-element.346, s32[1024]{0:T(1024)S(1)} %pad_clamp_fusion.3), kind=kCustom, calls=%fused_computation.clone.1 | custom fusion | bytes 1048640 | tf_op jit(solution)/shard_map/while/body/eval_jaxpr/jit(_take)/gather | solution.py:61
  80.7 0.6 fusion.53
  81.7 38.1 %psum.14 = f32[4,1000]{1,0:T(4,128)S(1)} all-reduce(f32[4,1000]{1,0:T(4,128)S(1)} %fusion.24), channel_id=1, replica_groups=mesh['grp'=4,'dev'=8] {'grp','dev'}, use_global_device_ids=true, to_apply=%region_6.7 | all-reduce | flops 4000 | bytes 32000 | tf_op jit(solution)/shard_map/psum | solution.py:82
  119.8 5.8 %while.31 = (s32[]{:T(128)}, f32[4,256]{1,0:T(4,128)S(1)}, f32[4,1000]{1,0:T(4,128)S(1)}, f32[4,3]{1,0:T(4,128)S(1)}, f32[4,3,256]{2,1,0:T(4,128)S(1)}, /*index=5*/f32[3,1000]{1,0:T(4,128)S(1)}, s32[]{:T(128)}, s32[]{:T(128)}) while((s32[]{:T(128)}, f32[4,256]{1,0:T(4,128)S(1)}, f32[4,1000]{1,0:T(4,128)S(1)}, f32[4,3]{1,0:T(4,128)S(1)}, ...), condition=%wide.region_9.10_spmd, body=%wide.region_7.9_spmd.sunk | while | flops 5120514 | bytes 6216429 | solution.py:88
  119.9 0.5 broadcast_subtract_fusion.2
  120.4 0.8 fusion.55
  121.4 0.5 broadcast_subtract_fusion.2
  121.8 0.8 fusion.55
  122.8 0.5 broadcast_subtract_fusion.2
  123.3 0.8 fusion.55
  124.3 0.5 broadcast_subtract_fusion.2
  124.7 0.8 fusion.55
  125.6 0.6 copy-done.2
  126.2 9.0 %while.32 = (s32[]{:T(128)}, f32[4,4,4,128,128]{4,3,2,1,0:T(8,128)}, bf16[4,256,512]{1,2,0:T(8,128)(2,1)S(1)}, f32[4,256]{1,0:T(4,128)S(1)}, f32[4,256]{1,0:T(4,128)S(1)}, /*index=5*/s32[]{:T(128)}) while((s32[]{:T(128)}, f32[4,4,4,128,128]{4,3,2,1,0:T(8,128)}, bf16[4,256,512]{1,2,0:T(8,128)(2,1)S(1)}, f32[4,256]{1,0:T(4,128)S(1)}, ...), condition=%wide.region_11.12_spmd, body=%wide.region_10.11_spmd.sunk | while | flops 271187968 | bytes 7870553 | solution.py:98
  126.6 0.4 convolution_bitcast_fusion.3
  127.1 0.3 copy.87
  127.4 1.1 constant_dynamic-update-slice_fusion.2
  128.9 0.4 convolution_bitcast_fusion.3
  129.3 0.3 copy.87
  129.6 1.1 constant_dynamic-update-slice_fusion.2
  131.2 0.4 convolution_bitcast_fusion.3
  131.6 0.3 copy.87
  131.9 1.1 constant_dynamic-update-slice_fusion.2
  133.4 0.4 convolution_bitcast_fusion.3
  133.8 0.3 copy.87
  134.2 1.1 constant_dynamic-update-slice_fusion.2
  135.2 11.4 %scatter_custom_fusion = f32[64,16384]{1,0:T(8,128)} fusion(s32[64]{0:T(128)S(1)} %reshape.178, f32[8,8,128,128]{3,2,1,0:T(8,128)} %bitcast.155, f32[]{:T(128)} %constant.70.clone.1), kind=kCustom, calls=%fused_computation.44 | custom fusion | flops 1048576 | bytes 8388612 | tf_op jit(solution)/shard_map/scatter-add | solution.py:100
  146.6 3.9 %convert_bitcast_fusion = bf16[8,8,128,128]{3,1,2,0:T(8,128)(2,1)} fusion(f32[64,16384]{1,0:T(8,128)} %scatter_custom_fusion), kind=kLoop, calls=%fused_computation.49 | loop fusion | flops 1048576 | bytes 6291456 | tf_op jit(solution)/shard_map/reshape | solution.py:101
  150.5 5.9 %all-to-all-start.2 = ((bf16[8,8,128,128]{3,1,2,0:T(8,128)(2,1)}), bf16[8,8,128,128]{3,1,2,0:T(8,128)(2,1)S(1)}, u32[]{:S(2)}, u32[]{:S(2)}) async-start(bf16[8,8,128,128]{3,1,2,0:T(8,128)(2,1)} %convert_bitcast_fusion), calls=%async_computation.2 | async-start | bytes 4194304 | tf_op jit(solution)/shard_map/all_to_all | solution.py:103
  156.5 0.5 broadcast.133
  157.0 0.7 reduce.10
  157.7 45.4 %all-to-all-done.2 = bf16[8,8,128,128]{3,1,2,0:T(8,128)(2,1)S(1)} async-done(((bf16[8,8,128,128]{3,1,2,0:T(8,128)(2,1)}), bf16[8,8,128,128]{3,1,2,0:T(8,128)(2,1)S(1)}, u32[]{:S(2)}, u32[]{:S(2)}) %all-to-all-start.2) | async-done | bytes 2097184 | tf_op jit(solution)/shard_map/all_to_all | solution.py:103
  203.1 0.4 fusion.20
  203.5 16.5 %all-reduce.1 = bf16[8,16384]{1,0:T(8,128)(2,1)S(1)} all-reduce(f32[8,16384]{1,0:T(8,128)S(1)} %fusion.20), channel_id=1, replica_groups=mesh['grp'=4,'dev'=8] {'grp'}, use_global_device_ids=true, to_apply=%region_13.14 | all-reduce | flops 131072 | bytes 786432 | tf_op jit(solution)/shard_map/psum | solution.py:112
  219.9 0.7 copy.55
  (98 shorter events, 4.2 us)
Async XLA Ops:
  0.6 14.0 %copy-start = (bf16[8,128,128]{2,1,0:T(8,128)(2,1)S(1)}, bf16[8,128,128]{2,1,0:T(8,128)(2,1)}, u32[]{:S(2)}) copy-start(bf16[8,128,128]{2,1,0:T(8,128)(2,1)} %param.16) | copy-start | bytes 786436
  15.6 6.1 %copy-start.8 = (s32[4,16]{1,0:T(4,128)S(1)}, s32[4,16]{1,0:T(4,128)}, u32[]{:S(2)}) copy-start(s32[4,16]{1,0:T(4,128)} %param.18) | copy-start | bytes 772
  15.6 6.2 %copy-start.4 = (f32[3,4,256]{2,1,0:T(4,128)S(1)}, f32[3,4,256]{2,1,0:T(4,128)}, u32[]{:S(2)}) copy-start(f32[3,4,256]{2,1,0:T(4,128)} %param.20) | copy-start | bytes 36868
  15.6 6.2 %copy-start.1 = (bf16[4,256,512]{2,1,0:T(8,128)(2,1)S(1)}, bf16[4,256,512]{2,1,0:T(8,128)(2,1)}, u32[]{:S(2)}) copy-start(bf16[4,256,512]{2,1,0:T(8,128)(2,1)} %param.15) | copy-start | bytes 3145732
  17.2 5.1 %copy-start.3 = (f32[3,1000]{1,0:T(4,128)S(1)}, f32[3,1000]{1,0:T(4,128)}, u32[]{:S(2)}) copy-start(f32[3,1000]{1,0:T(4,128)} %param.23) | copy-start | bytes 36004
  17.2 5.1 %copy-start.9 = (s32[4]{0:T(128)S(1)}, s32[4]{0:T(128)}, u32[]{:S(2)}) copy-start(s32[4]{0:T(128)} %param.19) | copy-start | bytes 52
  17.2 51.6 %all-to-all-start.1 = ((bf16[8,8,128,128]{3,2,1,0:T(8,128)(2,1)}), bf16[8,8,128,128]{3,2,1,0:T(8,128)(2,1)}, u32[]{:S(2)}, u32[]{:S(2)}) async-start(bf16[8,8,128,128]{3,2,1,0:T(8,128)(2,1)} %broadcast_select_fusion), calls=%async_computation.1 | async-start | bytes 4194304 | tf_op jit(solution)/shard_map/all_to_all | solution.py:56
  68.8 12.6 %copy-start.5 = (f32[4,256]{1,0:T(4,128)S(1)}, f32[4,256]{1,0:T(4,128)}, u32[]{:S(2)}) copy-start(f32[4,256]{1,0:T(4,128)} %param.21) | copy-start | bytes 12292
  68.8 12.6 %copy-start.7 = (f32[4,256]{1,0:T(4,128)S(1)}, f32[4,256]{1,0:T(4,128)}, u32[]{:S(2)}) copy-start(f32[4,256]{1,0:T(4,128)} %param.22) | copy-start | bytes 12292
  81.3 38.5 %copy-start.6 = (f32[4,256]{1,0:T(4,128)}, f32[4,256]{1,0:T(4,128)S(1)}, u32[]{:S(2)}) copy-start(f32[4,256]{1,0:T(4,128)S(1)} %get-tuple-element.165) | copy-start | bytes 12292
  125.6 0.6 copy-start.2
  150.5 52.6 %all-to-all-start.2 = ((bf16[8,8,128,128]{3,1,2,0:T(8,128)(2,1)}), bf16[8,8,128,128]{3,1,2,0:T(8,128)(2,1)S(1)}, u32[]{:S(2)}, u32[]{:S(2)}) async-start(bf16[8,8,128,128]{3,1,2,0:T(8,128)(2,1)} %convert_bitcast_fusion), calls=%async_computation.2 | async-start | bytes 4194304 | tf_op jit(solution)/shard_map/all_to_all | solution.py:103
where the time goes:
time: 221 us
  waiting for transfers between devices  91.6 us (41%)
  blocking collectives  68.4 us (31%)
  other arithmetic  24 us (11%)
  local copies, waits for them, and re-layouts  20.4 us (9%)
  starting transfers between devices  10.4 us (5%)
  matrix products  4.75 us (2%)
    all_to_all x1, waiting for transfers between devices, on_device(): lax.all_to_all(picked, 'dev', split_axis=0, concat_axis=0, tiled=True)  46.2 us
    all_to_all x1, waiting for transfers between devices, on_device(): lax.all_to_all(outgoing, 'dev', split_axis=0, concat_axis=0, tiled=True)  45.4 us
    psum x1, blocking collectives, on_device(): multipoles = lax.psum(local_moments, ('grp', 'dev'))  38.1 us
    psum x1, blocking collectives, on_device(): total = lax.psum(owned, 'grp')  16.5 us
    all_to_all x1, blocking collectives, on_device(): lax.all_to_all(wanted, 'dev', split_axis=0, concat_axis=0, tiled=True)  13.8 us
    scatter-add x1, other arithmetic, on_device(): jax.ops.segment_sum(flat_terms, batch_blocks.reshape(-1), num_segments=po...  11.4 us
    gather x4, local copies, waits for them, and re-layouts, density_one(): blocks = jnp.take(fetched, needed, axis=0).reshape(rel, rel, tile, tile)  8.95 us
    all_to_all x1, starting transfers between devices, on_device(): lax.all_to_all(outgoing, 'dev', split_axis=0, concat_axis=0, tiled=True)  5.93 us
  transfers between devices with their start and end apart: 2, of which 2 were waited for; matrix products, arithmetic and copies ran while one was open for 1% of the time, Pallas kernels for 0%

commit v1 on v0

--- a/solution.py
+++ b/solution.py
@@ -79,7 +79,7 @@
     local_moments = jnp.dot(local_parts, onehot, precision=HIGH)
     centres = jnp.dot(atom_xyz, onehot.T, precision=HIGH)
     xc_part = point_weight * exchange_kernel * density_field
-    multipoles = lax.psum(local_moments, ("grp", "dev"))
+    multipoles = jnp.sum(lax.all_gather(local_moments, ("grp", "dev")), axis=0)
 
     def potential_one(args):
         centre, offset = args

time: 221 us -> 249 us (1.13)
  blocking collectives: 68.4 us -> 100 us
    all_gather x0 -> x1, blocking collectives: none -> 69.6 us  [on_device(): multipoles = jnp.sum(lax.all_gather(local_moments, ('grp', 'dev')), axis=0)]
    psum x1 -> x0, blocking collectives: 38.1 us -> none  [on_device(): multipoles = lax.psum(local_moments, ('grp', 'dev'))]
where the time goes in v1:
time: 249 us; the launch traced here: 248 us
  blocking collectives  100 us (40%)
  waiting for transfers between devices  89.9 us (36%)
  other arithmetic  24.1 us (10%)
  local copies, waits for them, and re-layouts  20.4 us (8%)
  starting transfers between devices  8.07 us (3%)
  matrix products  4.75 us (2%)
    all_gather x1, blocking collectives, on_device(): multipoles = jnp.sum(lax.all_gather(local_moments, ('grp', 'dev')), axis=0)  69.6 us
    all_to_all x1, waiting for transfers between devices, on_device(): lax.all_to_all(picked, 'dev', split_axis=0, concat_axis=0, tiled=True)  46.2 us
    all_to_all x1, waiting for transfers between devices, on_device(): lax.all_to_all(outgoing, 'dev', split_axis=0, concat_axis=0, tiled=True)  43.7 us
    psum x1, blocking collectives, on_device(): total = lax.psum(owned, 'grp')  16.5 us
    all_to_all x1, blocking collectives, on_device(): lax.all_to_all(wanted, 'dev', split_axis=0, concat_axis=0, tiled=True)  13.8 us
    scatter-add x1, other arithmetic, on_device(): jax.ops.segment_sum(flat_terms, batch_blocks.reshape(-1), num_segments=po...  11.4 us
    gather x4, local copies, waits for them, and re-layouts, density_one(): blocks = jnp.take(fetched, needed, axis=0).reshape(rel, rel, tile, tile)  8.95 us
    dynamic_update_slice x8, local copies, waits for them, and re-layouts, on_device(): terms = lax.map(both_one, (basis_values, xc_part, hartree_part))  5.63 us
  transfers between devices with their start and end apart: 2, of which 2 were waited for; matrix products, arithmetic and copies ran while one was open for 1% of the time, Pallas kernels for 0%

profile of v1, /device:TPU:0, one launch (start us, length us, event | category | flops | bytes accessed | tf_op | source)
XLA Modules:
  0.0 248.4 jit_solution(6959412252945136319)
XLA Ops:
  0.6 13.8 %all_to_all.20 = s32[8,1,8]{2,1,0:T(1,128)S(1)} all-to-all(s32[8,1,8]{2,1,0:T(1,128)} %bitcast.170), channel_id=1, replica_groups=mesh['grp'=4,'dev'=8] {'dev'}, dimensions={0} | all-to-all | bytes 512 | tf_op jit(solution)/shard_map/all_to_all | solution.py:104
  14.6 1.0 gather_fusion.1
  15.6 1.6 broadcast_select_fusion
  17.2 4.5 %all-to-all-start.1 = ((bf16[8,8,128,128]{3,2,1,0:T(8,128)(2,1)}), bf16[8,8,128,128]{3,2,1,0:T(8,128)(2,1)}, u32[]{:S(2)}, u32[]{:S(2)}) async-start(bf16[8,8,128,128]{3,2,1,0:T(8,128)(2,1)} %broadcast_select_fusion), calls=%async_computation.1 | async-start | bytes 4194304 | tf_op jit(solution)/shard_map/all_to_all | solution.py:56
  21.8 0.5 copy.53
  22.5 46.2 %all-to-all-done.1 = bf16[8,8,128,128]{3,2,1,0:T(8,128)(2,1)} async-done(((bf16[8,8,128,128]{3,2,1,0:T(8,128)(2,1)}), bf16[8,8,128,128]{3,2,1,0:T(8,128)(2,1)}, u32[]{:S(2)}, u32[]{:S(2)}) %all-to-all-start.1) | async-done | bytes 2097184 | tf_op jit(solution)/shard_map/all_to_all | solution.py:56
  68.8 12.6 %while.30 = (s32[]{:T(128)}, f32[4,256]{1,0:T(4,128)S(1)}, bf16[4,256,512]{1,2,0:T(8,128)(2,1)S(1)}, s32[4,16]{1,0:T(4,128)S(1)}, bf16[64,128,128]{2,1,0:T(8,128)(2,1)}, /*index=5*/s32[]{:T(128)}, s32[]{:T(128)}) while((s32[]{:T(128)}, f32[4,256]{1,0:T(4,128)S(1)}, bf16[4,256,512]{1,2,0:T(8,128)(2,1)S(1)}, s32[4,16]{1,0:T(4,128)S(1)}, ...), condition=%wide.region_1.2_spmd, body=%wide.region_0.1_spmd.sunk | while | flops 134874000 | bytes 2629349 | solution.py:66
  69.0 2.2 gather_fusion
  71.3 0.6 fusion.52
  72.2 2.2 gather_fusion
  74.4 0.6 fusion.52
  75.3 2.2 gather_fusion
  77.6 0.6 fusion.52
  78.5 2.2 gather_fusion
  80.7 0.6 fusion.52
  81.7 69.6 %all-gather.1 = f32[32,4,1000]{2,1,0:T(4,128)S(1)} all-gather(f32[1,4,1000]{2,1,0:T(4,128)S(1)} %convolution_bitcast_fusion.2), channel_id=2, replica_groups=mesh['grp'=4,'dev'=8] {'grp','dev'}, dimensions={0}, use_global_device_ids=true | all-gather | bytes 528000 | tf_op jit(solution)/shard_map/all_gather | solution.py:82
  151.5 5.8 %while.31 = (s32[]{:T(128)}, f32[4,256]{1,0:T(4,128)S(1)}, f32[4,1000]{1,0:T(4,128)S(1)}, f32[4,3]{1,0:T(4,128)S(1)}, f32[4,3,256]{2,1,0:T(4,128)S(1)}, /*index=5*/f32[3,1000]{1,0:T(4,128)S(1)}, s32[]{:T(128)}, s32[]{:T(128)}) while((s32[]{:T(128)}, f32[4,256]{1,0:T(4,128)S(1)}, f32[4,1000]{1,0:T(4,128)S(1)}, f32[4,3]{1,0:T(4,128)S(1)}, ...), condition=%wide.region_9.10_spmd, body=%wide.region_7.9_spmd.sunk | while | flops 5120514 | bytes 6216429 | solution.py:88
  151.6 0.5 broadcast_subtract_fusion.2
  152.1 0.8 fusion.54
  153.1 0.5 broadcast_subtract_fusion.2
  153.5 0.8 fusion.54
  154.5 0.5 broadcast_subtract_fusion.2
  155.0 0.8 fusion.54
  156.0 0.5 broadcast_subtract_fusion.2
  156.4 0.8 fusion.54
  157.3 0.6 copy-done.2
  157.9 9.0 %while.32 = (s32[]{:T(128)}, f32[4,4,4,128,128]{4,3,2,1,0:T(8,128)}, bf16[4,256,512]{1,2,0:T(8,128)(2,1)S(1)}, f32[4,256]{1,0:T(4,128)S(1)}, f32[4,256]{1,0:T(4,128)S(1)}, /*index=5*/s32[]{:T(128)}) while((s32[]{:T(128)}, f32[4,4,4,128,128]{4,3,2,1,0:T(8,128)}, bf16[4,256,512]{1,2,0:T(8,128)(2,1)S(1)}, f32[4,256]{1,0:T(4,128)S(1)}, ...), condition=%wide.region_11.12_spmd, body=%wide.region_10.11_spmd.sunk | while | flops 271187968 | bytes 7870553 | solution.py:98
  158.3 0.4 convolution_bitcast_fusion.4
  158.8 0.3 copy.88
  159.1 1.1 constant_dynamic-update-slice_fusion.2
  160.6 0.4 convolution_bitcast_fusion.4
  161.0 0.3 copy.88
  161.4 1.1 constant_dynamic-update-slice_fusion.2
  162.9 0.4 convolution_bitcast_fusion.4
  163.3 0.3 copy.88
  163.6 1.1 constant_dynamic-update-slice_fusion.2
  165.1 0.4 convolution_bitcast_fusion.4
  165.5 0.3 copy.88
  165.9 1.1 constant_dynamic-update-slice_fusion.2
  166.9 11.4 %scatter_custom_fusion = f32[64,16384]{1,0:T(8,128)} fusion(s32[64]{0:T(128)S(1)} %reshape.178, f32[8,8,128,128]{3,2,1,0:T(8,128)} %bitcast.157, f32[]{:T(128)} %constant.70.clone.1), kind=kCustom, calls=%fused_computation.44 | custom fusion | flops 1048576 | bytes 8388612 | tf_op jit(solution)/shard_map/scatter-add | solution.py:100
  178.4 3.9 %convert_bitcast_fusion = bf16[8,8,128,128]{3,1,2,0:T(8,128)(2,1)} fusion(f32[64,16384]{1,0:T(8,128)} %scatter_custom_fusion), kind=kLoop, calls=%fused_computation.49 | loop fusion | flops 1048576 | bytes 6291456 | tf_op jit(solution)/shard_map/reshape | solution.py:101
  182.2 3.6 %all-to-all-start.2 = ((bf16[8,8,128,128]{3,1,2,0:T(8,128)(2,1)}), bf16[8,8,128,128]{3,1,2,0:T(8,128)(2,1)S(1)}, u32[]{:S(2)}, u32[]{:S(2)}) async-start(bf16[8,8,128,128]{3,1,2,0:T(8,128)(2,1)} %convert_bitcast_fusion), calls=%async_computation.2 | async-start | bytes 4194304 | tf_op jit(solution)/shard_map/all_to_all | solution.py:103
  185.8 0.5 broadcast.133
  186.4 0.7 reduce.11
  187.1 43.7 %all-to-all-done.2 = bf16[8,8,128,128]{3,1,2,0:T(8,128)(2,1)S(1)} async-done(((bf16[8,8,128,128]{3,1,2,0:T(8,128)(2,1)}), bf16[8,8,128,128]{3,1,2,0:T(8,128)(2,1)S(1)}, u32[]{:S(2)}, u32[]{:S(2)}) %all-to-all-start.2) | async-done | bytes 2097184 | tf_op jit(solution)/shard_map/all_to_all | solution.py:103
  230.8 0.4 fusion.20
  231.2 16.5 %all-reduce.1 = bf16[8,16384]{1,0:T(8,128)(2,1)S(1)} all-reduce(f32[8,16384]{1,0:T(8,128)S(1)} %fusion.20), channel_id=1, replica_groups=mesh['grp'=4,'dev'=8] {'grp'}, use_global_device_ids=true, to_apply=%region_13.14 | all-reduce | flops 131072 | bytes 786432 | tf_op jit(solution)/shard_map/psum | solution.py:112
  247.7 0.7 copy.55
  (99 shorter events, 4.2 us)
Async XLA Ops:
  0.6 14.0 %copy-start = (bf16[8,128,128]{2,1,0:T(8,128)(2,1)S(1)}, bf16[8,128,128]{2,1,0:T(8,128)(2,1)}, u32[]{:S(2)}) copy-start(bf16[8,128,128]{2,1,0:T(8,128)(2,1)} %param.16) | copy-start | bytes 786436
  15.6 6.1 %copy-start.8 = (s32[4,16]{1,0:T(4,128)S(1)}, s32[4,16]{1,0:T(4,128)}, u32[]{:S(2)}) copy-start(s32[4,16]{1,0:T(4,128)} %param.18) | copy-start | bytes 772
  15.6 6.2 %copy-start.4 = (f32[3,4,256]{2,1,0:T(4,128)S(1)}, f32[3,4,256]{2,1,0:T(4,128)}, u32[]{:S(2)}) copy-start(f32[3,4,256]{2,1,0:T(4,128)} %param.20) | copy-start | bytes 36868
  17.2 4.6 %copy-start.1 = (bf16[4,256,512]{2,1,0:T(8,128)(2,1)S(1)}, bf16[4,256,512]{2,1,0:T(8,128)(2,1)}, u32[]{:S(2)}) copy-start(bf16[4,256,512]{2,1,0:T(8,128)(2,1)} %param.15) | copy-start | bytes 3145732
  17.2 5.1 %copy-start.3 = (f32[3,1000]{1,0:T(4,128)S(1)}, f32[3,1000]{1,0:T(4,128)}, u32[]{:S(2)}) copy-start(f32[3,1000]{1,0:T(4,128)} %param.23) | copy-start | bytes 36004
  17.2 5.1 %copy-start.9 = (s32[4]{0:T(128)S(1)}, s32[4]{0:T(128)}, u32[]{:S(2)}) copy-start(s32[4]{0:T(128)} %param.19) | copy-start | bytes 52
  17.2 51.6 %all-to-all-start.1 = ((bf16[8,8,128,128]{3,2,1,0:T(8,128)(2,1)}), bf16[8,8,128,128]{3,2,1,0:T(8,128)(2,1)}, u32[]{:S(2)}, u32[]{:S(2)}) async-start(bf16[8,8,128,128]{3,2,1,0:T(8,128)(2,1)} %broadcast_select_fusion), calls=%async_computation.1 | async-start | bytes 4194304 | tf_op jit(solution)/shard_map/all_to_all | solution.py:56
  68.8 12.6 %copy-start.5 = (f32[4,256]{1,0:T(4,128)S(1)}, f32[4,256]{1,0:T(4,128)}, u32[]{:S(2)}) copy-start(f32[4,256]{1,0:T(4,128)} %param.21) | copy-start | bytes 12292
  68.8 12.6 %copy-start.7 = (f32[4,256]{1,0:T(4,128)S(1)}, f32[4,256]{1,0:T(4,128)}, u32[]{:S(2)}) copy-start(f32[4,256]{1,0:T(4,128)} %param.22) | copy-start | bytes 12292
  81.3 70.2 %copy-start.6 = (f32[4,256]{1,0:T(4,128)}, f32[4,256]{1,0:T(4,128)S(1)}, u32[]{:S(2)}) copy-start(f32[4,256]{1,0:T(4,128)S(1)} %get-tuple-element.165) | copy-start | bytes 12292
  157.3 0.6 copy-start.2
  182.2 48.6 %all-to-all-start.2 = ((bf16[8,8,128,128]{3,1,2,0:T(8,128)(2,1)}), bf16[8,8,128,128]{3,1,2,0:T(8,128)(2,1)S(1)}, u32[]{:S(2)}, u32[]{:S(2)}) async-start(bf16[8,8,128,128]{3,1,2,0:T(8,128)(2,1)} %convert_bitcast_fusion), calls=%async_computation.2 | async-start | bytes 4194304 | tf_op jit(solution)/shard_map/all_to_all | solution.py:103
